TPU v7x, 32 devices: a whole 2x2x4 slice. The times are simulated.
32 devices in a mesh: trade: 4 (over z), node: 8 (over y, x, core).
Axes of the slice: x: 2, y: 2, z: 4, core: 2. Of those that a mesh axis runs over, the one named last changes fastest.
Arguments:
- values_in: float32 [1024, 16384], P('trade', 'node'), may hold values from 0 to 1
- prob_up: float32 [16, 16384], P(None, 'node'), may hold values from 0.1 to 0.3
- prob_down: float32 [16, 16384], P(None, 'node'), may hold values from 0.1 to 0.3
- discount: float32 [16, 16384], P(None, 'node'), may hold values from 0.9 to 1
- swap_rate: float32 [16, 16384], P(None, 'node'), may hold values from -3 to 3
- annuity: float32 [16, 16384], P(None, 'node'), may hold values from 0.5 to 2
- state_price: float32 [16384], P('node'), may hold values from 3.0517578e-05 to 0.00012207031
- exercise_step: int32 [1024, 4], P('trade'), may hold values from 0 to 15
- strike_bucket: int32 [1024], P('trade'), may hold values from 0 to 63
- notional_sign: int32 [1024], P('trade'), may hold values from 0 to 1
- strike_table: float32 [64], replicated, may hold values from -0.5 to 0.5
Outputs:
- values_out: float32 [1024, 16384], P(('trade', 'node'))
- prices: float32 [1024], P(('trade', 'node'))
- portfolio: float32 [], replicated
All inputs are finite; a program needn't handle non-finite values.
Results may differ from a plain program's by a relative error of at most 0.0003.
Values sent between devices are 32-bit elements; how exact they have to be, the bound alone decides.
A program may use at most 128 MiB of HBM per device.

v0:
```python
import jax
import jax.numpy as jnp
from jax import lax
from jax.sharding import PartitionSpec as P


def strikes_of(bucket, strike_table):
    levels = lax.broadcasted_iota(jnp.int32, (1, strike_table.shape[0]), 1)
    return jnp.sum(
        jnp.where(
            bucket[:, None] == levels, strike_table[None, :], jnp.zeros((), strike_table.dtype)
        ),
        axis=1,
    )


def roll_once(padded, prob_up, prob_down, discount_row):
    middle = 1.0 - prob_up - prob_down
    return discount_row * (
        prob_up * padded[:, 2:] + middle * padded[:, 1:-1] + prob_down * padded[:, :-2]
    )


def exercise(values, active, strike, signs, swap_row, annuity_row):
    payoff = signs[:, None] * annuity_row[None, :] * (swap_row[None, :] - strike[:, None])
    return jnp.where(active[:, None], jnp.maximum(values, payoff), values)


def stack_lattice(prob_up, prob_down, discount, swap_rate, annuity, state_price, first_step):
    span = prob_up.shape[0] - first_step
    spread_price = jnp.broadcast_to(state_price[None, :], (span, state_price.shape[0]))
    return jnp.stack([prob_up, prob_down, discount, swap_rate, annuity, spread_price])


def to_trade_rows(values):
    node_count = lax.axis_size("node")
    node_dev = values.shape[1]
    row_count = values.shape[0] // node_count
    blocks = values.reshape(node_count, row_count, node_dev)
    moved = lax.all_to_all(blocks, "node", split_axis=0, concat_axis=2, tiled=True)
    return moved.reshape(row_count, node_dev * node_count)


def roll_back(values, lattice, exercise_step, strike, signs, split_step, step_count):
    row_count = values.shape[0]
    first_row = lax.axis_index("node") * row_count
    my_dates = lax.dynamic_slice_in_dim(exercise_step, first_row, row_count, 0)
    my_strike = lax.dynamic_slice_in_dim(strike, first_row, row_count, 0)
    my_signs = lax.dynamic_slice_in_dim(signs, first_row, row_count, 0)
    for step in range(split_step, step_count):
        local_step = step - split_step
        padded = jnp.pad(values, ((0, 0), (1, 1)))
        values = roll_once(
            padded, lattice[0, local_step], lattice[1, local_step], lattice[2, local_step]
        )
        active = jnp.any(my_dates == step, axis=1)
        values = exercise(
            values, active, my_strike, my_signs, lattice[3, local_step], lattice[4, local_step]
        )
    prices = jnp.sum(values * lattice[5, 0][None, :], axis=1)
    return (values, prices)


def local(
    values_in,
    prob_up,
    prob_down,
    discount,
    swap_rate,
    annuity,
    state_price,
    exercise_step,
    strike_bucket,
    notional_sign,
    strike_table,
):
    step_count = prob_up.shape[0]
    strike = strikes_of(strike_bucket, strike_table)
    signs = (2 * notional_sign - 1).astype(jnp.float32)
    values = to_trade_rows(values_in)
    local_lattice = stack_lattice(prob_up, prob_down, discount, swap_rate, annuity, state_price, 0)
    lattice = lax.all_gather(local_lattice, "node", axis=2, tiled=True)
    values, prices = roll_back(values, lattice, exercise_step, strike, signs, 0, step_count)
    portfolio = lax.psum(jnp.sum(prices), ("trade", "node")) / values_in.shape[0]
    return (values, prices, portfolio)


def solution(mesh):
    in_specs = (
        P("trade", "node"),
        P(None, "node"),
        P(None, "node"),
        P(None, "node"),
        P(None, "node"),
        P(None, "node"),
        P("node"),
        P("trade", None),
        P("trade"),
        P("trade"),
        P(),
    )
    out_specs = (P(("trade", "node"), None), P(("trade", "node")), P())
    return jax.shard_map(local, mesh=mesh, in_specs=in_specs, out_specs=out_specs, check_vma=False)
```

profile of v0, /device:TPU:0, one launch (start us, length us, event | category | flops | bytes accessed | tf_op | source)
XLA Modules:
  0.0 175.1 jit_solution(9109322315187114257)
XLA Ops:
  7.2 0.0 all-gather.2.cloned.1.call-start
  7.2 0.9 bitcast_dynamic-update-slice_fusion.4
  8.1 0.9 bitcast_dynamic-update-slice_fusion.3
  9.0 0.9 bitcast_dynamic-update-slice_fusion.2
  10.0 0.9 bitcast_dynamic-update-slice_fusion.1
  10.9 0.9 bitcast_dynamic-update-slice_fusion
  11.8 0.7 broadcast_dynamic-update-slice_fusion
  12.5 0.0 copy-start.1
  12.5 0.9 copy-done.1
  13.4 0.0 all-gather.2.cloned.1.call-update
  13.4 0.0 copy-start.2
  13.4 0.0 copy-start.3
  13.5 0.0 copy-start.5
  13.5 0.0 copy-start.4
  13.5 5.3 %all-to-all-start = ((f32[8,32,2048]{2,1,0:T(8,128)}), f32[8,32,2048]{2,1,0:T(8,128)S(1)}, u32[]{:S(2)}, u32[]{:S(2)}) async-start(f32[8,32,2048]{2,1,0:T(8,128)} %bitcast.102), calls=%async_computation | async-start | bytes 4194304 | tf_op jit(solution)/shard_map/all_to_all | solution.py:40
  18.8 0.0 copy-done.2
  18.8 0.1 dynamic_slice.10
  18.9 0.0 copy-done.3
  18.9 0.0 copy-done.5
  18.9 0.1 select_reduce_fusion
  19.0 0.1 dynamic_slice.11
  19.1 0.0 copy-done.4
  19.1 0.1 compare_reduce_fusion.15
  19.2 34.6 %all-to-all-done = f32[8,32,2048]{2,1,0:T(8,128)S(1)} async-done(((f32[8,32,2048]{2,1,0:T(8,128)}), f32[8,32,2048]{2,1,0:T(8,128)S(1)}, u32[]{:S(2)}, u32[]{:S(2)}) %all-to-all-start) | async-done | bytes 2097184 | tf_op jit(solution)/shard_map/all_to_all | solution.py:40
  53.8 0.0 copy-start
  53.8 1.3 copy-done
  55.1 2.2 %copy.17 = f32[4,8,8,2048]{3,1,2,0:T(8,128)S(1)} copy(f32[4,8,8,2048]{3,1,0,2:T(8,128)} %bitcast.101) | data formatting | bytes 4194304
  57.3 19.5 %all-gather.2.cloned.1.call-done = f32[6,16,16384]{2,1,0:T(8,128)} async-done(((f32[6,16,2048]{2,1,0:T(8,128)}), f32[6,16,16384]{2,1,0:T(8,128)}) %all-gather.2.cloned.1.call-update) | async-done | bytes 6291472 | tf_op jit(solution)/shard_map/all_gather | solution.py:82
  76.8 5.8 %fusion.2 = (f32[1,1,16384]{2,1,0:T(1,128)S(1)}, f32[1,1,16384]{2,1,0:T(1,128)S(1)}, f32[1,1,16384]{2,1,0:T(1,128)S(1)}, f32[1,1,16384]{2,1,0:T(1,128)S(1)}, f32...) fusion(f32[6,16,16384]{2,1,0:T(8,128)} %all-gather.2.cloned.1.c, ...), kind=kLoop, calls=%fused_computation.62 | loop fusion | bytes 2490368 | tf_op jit(solution)/shard_map/slice | solution.py:54
  82.7 5.7 %fusion.3 = (f32[1,1,16384]{2,1,0:T(1,128)S(1)}, f32[1,1,16384]{2,1,0:T(1,128)S(1)}, f32[1,1,16384]{2,1,0:T(1,128)S(1)}, f32[1,1,16384]{2,1,0:T(1,128)S(1)}, f32...) fusion(f32[6,16,16384]{2,1,0:T(8,128)} %all-gather.2.cloned.1.c, ...), kind=kLoop, calls=%fused_computation.63 | loop fusion | bytes 2490368 | tf_op jit(solution)/shard_map/slice | solution.py:54
  88.4 5.5 %fusion.1 = (f32[1,1,16384]{2,1,0:T(1,128)S(1)}, f32[1,1,16384]{2,1,0:T(1,128)S(1)}, f32[1,1,16384]{2,1,0:T(1,128)S(1)}, f32[1,1,16384]{2,1,0:T(1,128)S(1)}, f32...) fusion(f32[6,16,16384]{2,1,0:T(8,128)} %all-gather.2.cloned.1.c, ...), kind=kLoop, calls=%fused_computation.61 | loop fusion | bytes 2490368 | tf_op jit(solution)/shard_map/slice | solution.py:54
  94.1 6.1 %fusion = (f32[1,1,16384]{2,1,0:T(1,128)S(1)}, f32[1,1,16384]{2,1,0:T(1,128)S(1)}, f32[1,1,16384]{2,1,0:T(1,128)S(1)}, f32[1,1,16384]{2,1,0:T(1,128)S(1)}, f32[1...) fusion(f32[6,16,16384]{2,1,0:T(8,128)} %all-gather.2.cloned.1.c, ...), kind=kLoop, calls=%fused_computation.60 | loop fusion | bytes 2490368 | tf_op jit(solution)/shard_map/slice | solution.py:54
  100.2 2.1 %fusion.4 = (f32[1,1,16384]{2,1,0:T(1,128)S(1)}, f32[1,1,16384]{2,1,0:T(1,128)S(1)}, f32[1,1,16384]{2,1,0:T(1,128)S(1)}, f32[1,1,16384]{2,1,0:T(1,128)S(1)}, f32[1,1,16384]{2,1,0:T(1,128)S(1)}) fusion(f32[6,16,16384]{2,1,0:T(8,128)} %all-gather.2.cloned.1.call-done), kind=kLoop, calls=%fused_computation.64 | loop fusion | bytes 655360 | tf_op jit(solution)/shard_map/slice | solution.py:54
  102.4 1.4 maximum_select_fusion.15
  103.8 1.4 maximum_select_fusion.14
  105.2 1.4 maximum_select_fusion.13
  106.6 1.4 maximum_select_fusion.12
  107.9 1.6 maximum_select_fusion.11
  109.5 1.4 maximum_select_fusion.10
  110.9 1.4 maximum_select_fusion.9
  112.3 1.4 maximum_select_fusion.8
  113.7 1.4 maximum_select_fusion.7
  115.1 1.4 maximum_select_fusion.6
  116.5 1.4 maximum_select_fusion.5
  117.9 1.4 maximum_select_fusion.4
  119.3 1.4 maximum_select_fusion.3
  120.6 1.6 maximum_select_fusion.2
  122.2 1.4 maximum_select_fusion.1
  123.6 3.4 %multiply_reduce_fusion = (f32[]{:T(128)}, f32[32]{0:T(128)}, f32[32,16384]{1,0:T(8,128)}) fusion(f32[16384]{0:T(1024)S(1)} %bitcast.169, f32[32]{0:T(128)S(1)} %dynamic_slice.11, f32[16384]{0:T(1024)S(1)} %bitcast.170, f32[16384]{0:T(1024)S(1)} %bitcast.171, f32[32]{0:T(128)S(1)} %dynamic_slice.10, f32[16384]{0:T(1024)S(1)} %bitcast.108, ...), kind=kLoop, calls=%fused_computation.16 | loop fusion | flops 7339999 | bytes 4653476 | tf_op jit(solution)/shard_map/reduce_sum | solution.py:84
  127.0 39.5 %psum.7 = f32[]{:T(128)} all-reduce(f32[]{:T(128)} %get-tuple-element.3), channel_id=1, replica_groups=mesh['trade'=4,'node'=8] {'trade','node'}, use_global_device_ids=true, to_apply=%region_19.20 | all-reduce | flops 1 | bytes 8 | tf_op jit(solution)/shard_map/psum | solution.py:84
  (17 shorter events, 0.2 us)
Async XLA Ops:
  7.2 69.7 %all-gather.2.cloned.1.call-start = ((), (), s32[]{:S(2)}) async-start(), calls=%async_computation.1 | async-start | bytes 7077888 | tf_op jit(solution)/shard_map/all_gather | solution.py:82
  12.5 0.9 copy-start.1
  13.4 5.4 %copy-start.2 = (s32[256]{0:T(256)S(1)}, s32[256]{0:T(256)}, u32[]{:S(2)}) copy-start(s32[256]{0:T(256)} %param.20) | copy-start | bytes 3076
  13.4 5.5 %copy-start.3 = (s32[256]{0:T(256)S(1)}, s32[256]{0:T(256)}, u32[]{:S(2)}) copy-start(s32[256]{0:T(256)} %param.19) | copy-start | bytes 3076
  13.5 5.5 %copy-start.5 = (f32[64]{0:T(128)S(1)}, f32[64]{0:T(128)}, u32[]{:S(2)}) copy-start(f32[64]{0:T(128)} %param.21) | copy-start | bytes 772
  13.5 5.6 %copy-start.4 = (s32[256,4]{0,1:T(4,128)S(1)}, s32[256,4]{0,1:T(4,128)}, u32[]{:S(2)}) copy-start(s32[256,4]{0,1:T(4,128)} %param.18) | copy-start | bytes 12292
  13.5 40.3 %all-to-all-start = ((f32[8,32,2048]{2,1,0:T(8,128)}), f32[8,32,2048]{2,1,0:T(8,128)S(1)}, u32[]{:S(2)}, u32[]{:S(2)}) async-start(f32[8,32,2048]{2,1,0:T(8,128)} %bitcast.102), calls=%async_computation | async-start | bytes 4194304 | tf_op jit(solution)/shard_map/all_to_all | solution.py:40
  53.8 1.3 copy-start
Sparse Core Ops, SparseCore 0:
  13.6 63.2 all-gather.1
where the time goes:
time: 176 us; the launch traced here: 175 us
  waiting for transfers between devices  54.1 us (31%)
  blocking collectives  39.5 us (22%)
  local copies, waits for them, and re-layouts  35.1 us (20%)
  other arithmetic  24.9 us (14%)
  between operations  16.2 us (9%)
  starting transfers between devices  5.38 us (3%)
    psum x1, blocking collectives, local(): lax.psum(jnp.sum(prices), ('trade', 'node')) / values_in.shape[0]  39.5 us
    all_to_all x1, waiting for transfers between devices, to_trade_rows(): lax.all_to_all(blocks, 'node', split_axis=0, concat_axis=2, tiled=True)  34.6 us
    select_n x15, other arithmetic, exercise(): return jnp.where(active[:, None], jnp.maximum(values, payoff), values)  21.1 us
    all_gather x1, waiting for transfers between devices, local(): lattice = lax.all_gather(local_lattice, 'node', axis=2, tiled=True)  19.5 us
    slice x3, local copies, waits for them, and re-layouts, roll_back(): lattice[2, local_step]  14 us
    slice x2, local copies, waits for them, and re-layouts, roll_back(): lattice[0, local_step]  11.2 us
    unnamed x18, local copies, waits for them, and re-layouts  9.01 us
    all_to_all x1, starting transfers between devices, to_trade_rows(): lax.all_to_all(blocks, 'node', split_axis=0, concat_axis=2, tiled=True)  5.34 us
  transfers between devices with their start and end apart: 2, of which 2 were waited for; matrix products, arithmetic and copies ran while one was open for 1% of the time, Pallas kernels for 0%

commit v1 on v0

v1 whole, which is shorter than its diff:
```python
import functools

import jax
import jax.numpy as jnp
from jax import lax
from jax.experimental import pallas as pl
from jax.experimental.pallas import tpu as pltpu
from jax.sharding import PartitionSpec as P

MESH = pl.DeviceIdType.MESH
LANES = 128
SUB = 8


def kernel(
    node_count,
    trade_count,
    values_hbm,
    up_hbm,
    down_hbm,
    disc_hbm,
    swap_hbm,
    ann_hbm,
    price_ref,
    dates_ref,
    bucket_ref,
    sign_ref,
    table_ref,
    out_ref,
    small_ref,
    work,
    lattice,
    halo_values,
    halo_lattice,
    coef,
    rows_t,
    sign_b,
    strike_b,
    dates_b,
    z_send,
    z_recv,
    msg_send,
    msg_recv,
    in_sem,
    lat_sem,
    self_sem,
    hv_send,
    hv_recv,
    hl_send,
    hl_recv,
    block_send,
    block_recv,
    zs_sem,
    zr_sem,
    ms_sem,
    mr_sem,
):
    n = node_count
    me = lax.axis_index("node")
    my_trade = lax.axis_index("trade")
    trades, width = values_hbm.shape
    steps = up_hbm.shape[0]
    rows = trades // n
    cols = width // LANES
    tiles = 2 if rows % (2 * SUB) == 0 else 1
    group_rows = tiles * SUB
    lat_hbm = (up_hbm, down_hbm, disc_hbm, swap_hbm, ann_hbm)

    def peer(turn):
        mask = n - 1 - turn
        if n & (n - 1):
            return lax.rem(mask + n - me + n, n)
        total, bit = 0, 1
        while bit < n:
            total = total + lax.rem(me // bit + mask // bit, 2) * bit
            bit *= 2
        return total

    def in_copy(turn):
        at = pl.ds(pl.multiple_of(peer(turn) * rows, SUB), rows)
        return pltpu.make_async_copy(values_hbm.at[at], work.at[at], in_sem.at[turn])

    lat_copies = [
        pltpu.make_async_copy(lat_hbm[i], lattice.at[i], lat_sem.at[i]) for i in range(5)
    ]
    for copy in lat_copies:
        copy.start()
    for turn in range(n):
        in_copy(turn).start()

    barrier = pltpu.get_barrier_semaphore()
    for k in range(1, n):
        pl.semaphore_signal(
            barrier, inc=1, device_id={"node": lax.rem(me + k, n)}, device_id_type=MESH
        )
    for k in range(1, trade_count):
        pl.semaphore_signal(
            barrier,
            inc=1,
            device_id={"trade": lax.rem(my_trade + k, trade_count)},
            device_id_type=MESH,
        )
    pl.semaphore_wait(barrier, n - 1 + trade_count - 1)

    right, left = lax.rem(me + 1, n), lax.rem(me + n - 1, n)
    first, last = pl.ds(0, LANES), pl.ds(width - LANES, LANES)
    halos = []
    for side, (target, edge) in enumerate(((right, last), (left, first))):
        for i in range(5):
            halos.append(
                pltpu.make_async_remote_copy(
                    src_ref=lat_hbm[i].at[:, edge],
                    dst_ref=halo_lattice.at[side, i],
                    send_sem=hl_send.at[side, i],
                    recv_sem=hl_recv.at[side, i],
                    device_id={"node": target},
                    device_id_type=MESH,
                )
            )
        halos.append(
            pltpu.make_async_remote_copy(
                src_ref=values_hbm.at[:, edge],
                dst_ref=halo_values.at[side],
                send_sem=hv_send.at[side],
                recv_sem=hv_recv.at[side],
                device_id={"node": target},
                device_id_type=MESH,
            )
        )
    for copy in halos:
        copy.start()

    rows_t[0:4, :] = dates_ref[...].astype(jnp.float32)
    rows_t[4:5, :] = bucket_ref[...].astype(jnp.float32)
    rows_t[5:6, :] = sign_ref[...].astype(jnp.float32)
    rows_t[6:8, :] = jnp.zeros((2, trades), jnp.float32)
    per_trade = rows_t[...].T
    levels = lax.broadcasted_iota(jnp.int32, (trades, table_ref.shape[1]), 1).astype(jnp.float32)
    strike = jnp.sum(
        jnp.where(per_trade[:, 4:5] == levels, table_ref[...], 0.0), axis=1, keepdims=True
    )
    sign = 2.0 * per_trade[:, 5:6] - 1.0
    sign_b[...] = jnp.broadcast_to(sign, (trades, LANES))
    strike_b[...] = jnp.broadcast_to(sign * strike, (trades, LANES))
    for e in range(4):
        dates_b[e] = jnp.broadcast_to(per_trade[:, e : e + 1], (trades, LANES))

    for copy in lat_copies:
        copy.wait()

    def widen(row):
        return jnp.broadcast_to(row, (SUB, LANES))

    def spread(first_step, k, up, down, disc, swap, ann):
        rows_of = (disc * up, disc * (1.0 - up - down), disc * down, ann * swap, ann)
        for i, block in enumerate(rows_of):
            for r in range(SUB):
                coef[i, first_step + r, k] = widen(block[r : r + 1])

    def prepare(k, carry):
        at = pl.ds(pl.multiple_of(k * LANES, LANES), LANES)
        for first_step in range(0, steps, SUB):
            spread(
                first_step, k, *[lattice[i, pl.ds(first_step, SUB), at] for i in range(5)]
            )
        return carry

    lax.fori_loop(0, cols, prepare, 0)

    lane = lax.broadcasted_iota(jnp.int32, (SUB, LANES), 1)
    row = lax.broadcasted_iota(jnp.int32, (SUB, LANES), 0)
    on_right = lane < LANES // 2
    has_right = jnp.where(me < n - 1, 1.0, 0.0)
    has_left = jnp.where(me > 0, 1.0, 0.0)
    inside = jnp.where(lane < steps, has_right, jnp.where(lane >= LANES - steps, has_left, 0.0))

    for copy in halos:
        copy.wait()

    for first_step in range(0, steps, SUB):
        at = pl.ds(first_step, SUB)
        up, down, disc, swap, ann = [
            jnp.where(on_right, halo_lattice[1, i, at, :], halo_lattice[0, i, at, :])
            for i in range(5)
        ]
        spread(first_step, cols, up, down, disc * inside, swap, ann * inside)

    is_first, is_last = lane == 0, lane == LANES - 1
    count = cols + 1

    def group(base, offset, total, message):
        parts = []
        for u in range(tiles):
            at = pl.ds(pl.multiple_of(base + u * SUB, SUB), SUB)
            held = [work[at, pl.ds(k * LANES, LANES)] for k in range(cols)]
            held.append(
                inside * jnp.where(on_right, halo_values[1, at, :], halo_values[0, at, :])
            )
            parts.append(held)
        dates = [
            [
                dates_b[e, pl.ds(pl.multiple_of(base + u * SUB, SUB), SUB), :]
                for e in range(4)
            ]
            for u in range(tiles)
        ]
        signs = [
            sign_b[pl.ds(pl.multiple_of(base + u * SUB, SUB), SUB), :] for u in range(tiles)
        ]
        strikes = [
            strike_b[pl.ds(pl.multiple_of(base + u * SUB, SUB), SUB), :] for u in range(tiles)
        ]

        def step_once(step, flat):
            now = step.astype(jnp.float32)
            scale, shift = [], []
            for u in range(tiles):
                d = dates[u]
                active = (d[0] == now) | (d[1] == now) | (d[2] == now) | (d[3] == now)
                scale.append(jnp.where(active, signs[u], 0.0))
                shift.append(jnp.where(active, strikes[u], 0.0))
            old = [flat[u * count : (u + 1) * count] for u in range(tiles)]
            down = [[pltpu.roll(x, 1, 1) for x in old[u]] for u in range(tiles)]
            up = [[pltpu.roll(x, LANES - 1, 1) for x in old[u]] for u in range(tiles)]
            new = [[] for _ in range(tiles)]
            for k in range(count):
                a, b, c = coef[0, step, k], coef[1, step, k], coef[2, step, k]
                pay, ann = coef[3, step, k], coef[4, step, k]
                for u in range(tiles):
                    above = jnp.where(is_last, up[u][(k + 1) % count], up[u][k])
                    below = jnp.where(is_first, down[u][k - 1], down[u][k])
                    rolled = a * above + b * old[u][k] + c * below
                    new[u].append(jnp.maximum(rolled, scale[u] * pay - shift[u] * ann))
            return tuple(x for u in range(tiles) for x in new[u])

        flat = lax.fori_loop(0, steps, step_once, tuple(x for held in parts for x in held))
        for u in range(tiles):
            at = pl.ds(pl.multiple_of(base + u * SUB, SUB), SUB)
            priced = jnp.zeros((SUB, LANES), jnp.float32)
            for k in range(cols):
                x = flat[u * count + k]
                work[at, pl.ds(k * LANES, LANES)] = x
                priced = priced + x * widen(price_ref[:, pl.ds(k * LANES, LANES)])
            total = total + priced
            summed = jnp.sum(priced, axis=1, keepdims=True)
            message = message + jnp.where(lane == offset + u * SUB + row, summed, 0.0)
        return total, message

    my_cols = pl.ds(pl.multiple_of(me * width, LANES), width)

    def block_copy(turn):
        target = peer(turn)
        return pltpu.make_async_remote_copy(
            src_ref=work.at[pl.ds(pl.multiple_of(target * rows, SUB), rows)],
            dst_ref=out_ref.at[:, my_cols],
            send_sem=block_send.at[turn],
            recv_sem=block_recv.at[turn],
            device_id={"node": target},
            device_id_type=MESH,
        )

    zero = jnp.zeros((SUB, LANES), jnp.float32)

    def chunk(turn, total):
        start = peer(turn) * rows
        in_copy(turn).wait()

        def one(g, carry):
            return group(start + g * group_rows, g * group_rows, *carry)

        total, message = lax.fori_loop(0, rows // group_rows, one, (total, zero))
        msg_send[turn] = message

        @pl.when(turn < n - 1)
        def _():
            block_copy(turn).start()

        return total

    total = lax.fori_loop(0, n, chunk, zero)
    own = pltpu.make_async_copy(
        work.at[pl.ds(pl.multiple_of(me * rows, SUB), rows)], out_ref.at[:, my_cols], self_sem
    )
    own.start()

    z_send[...] = total
    z_copies = [
        pltpu.make_async_remote_copy(
            src_ref=z_send,
            dst_ref=z_recv.at[k - 1],
            send_sem=zs_sem.at[k - 1],
            recv_sem=zr_sem.at[k - 1],
            device_id={"trade": lax.rem(my_trade + k, trade_count)},
            device_id_type=MESH,
        )
        for k in range(1, trade_count)
    ]
    for copy in z_copies:
        copy.start()
    for k, copy in enumerate(z_copies):
        copy.wait()
        total = total + z_recv[k]
    summed = jnp.where(lane == LANES - 1, jnp.sum(total, axis=1, keepdims=True), 0.0)
    for turn in range(n):
        msg_send[turn] = msg_send[turn] + summed

    def msg_copy(turn):
        return pltpu.make_async_remote_copy(
            src_ref=msg_send.at[turn],
            dst_ref=msg_recv.at[turn],
            send_sem=ms_sem.at[turn],
            recv_sem=mr_sem.at[turn],
            device_id={"node": peer(turn)},
            device_id_type=MESH,
        )

    own.wait()
    for turn in range(n - 1):
        msg_copy(turn).start()
    result = msg_send[n - 1]
    for turn in range(n - 1):
        msg_copy(turn).wait()
        result = result + msg_recv[turn]
    small_ref[...] = jnp.sum(result, axis=0, keepdims=True)
    for turn in range(n - 1):
        block_copy(turn).wait()


def local(
    node_count,
    trade_count,
    values_in,
    prob_up,
    prob_down,
    discount,
    swap_rate,
    annuity,
    state_price,
    exercise_step,
    strike_bucket,
    notional_sign,
    strike_table,
):
    trades, width = values_in.shape
    steps = prob_up.shape[0]
    n = node_count
    rows = trades // n
    f32 = jnp.float32
    dma = pltpu.SemaphoreType.DMA
    any_spec = pl.BlockSpec(memory_space=pl.ANY)
    vmem_spec = pl.BlockSpec(memory_space=pltpu.VMEM)
    values, small = pl.pallas_call(
        functools.partial(kernel, n, trade_count),
        out_shape=(
            jax.ShapeDtypeStruct((rows, width * n), f32),
            jax.ShapeDtypeStruct((1, LANES), f32),
        ),
        in_specs=[any_spec] * 6 + [vmem_spec] * 5,
        out_specs=(vmem_spec, vmem_spec),
        scratch_shapes=[
            pltpu.VMEM((trades, width), f32),
            pltpu.VMEM((5, steps, width), f32),
            pltpu.VMEM((2, trades, LANES), f32),
            pltpu.VMEM((2, 5, steps, LANES), f32),
            pltpu.VMEM((5, steps, width // LANES + 1, SUB, LANES), f32),
            pltpu.VMEM((SUB, trades), f32),
            pltpu.VMEM((trades, LANES), f32),
            pltpu.VMEM((trades, LANES), f32),
            pltpu.VMEM((4, trades, LANES), f32),
            pltpu.VMEM((SUB, LANES), f32),
            pltpu.VMEM((trade_count - 1, SUB, LANES), f32),
            pltpu.VMEM((n, SUB, LANES), f32),
            pltpu.VMEM((n - 1, SUB, LANES), f32),
            dma((n,)),
            dma((5,)),
            dma,
            dma((2,)),
            dma((2,)),
            dma((2, 5)),
            dma((2, 5)),
            dma((n - 1,)),
            dma((n - 1,)),
            dma((trade_count - 1,)),
            dma((trade_count - 1,)),
            dma((n - 1,)),
            dma((n - 1,)),
        ],
        compiler_params=pltpu.CompilerParams(
            collective_id=0, has_side_effects=True, vmem_limit_bytes=32 * 1024 * 1024
        ),
    )(
        values_in,
        prob_up,
        prob_down,
        discount,
        swap_rate,
        annuity,
        state_price.reshape(1, width),
        exercise_step.T,
        strike_bucket.reshape(1, trades),
        notional_sign.reshape(1, trades),
        strike_table.reshape(1, strike_table.shape[0]),
    )
    return (values, small[0, :rows], small[0, LANES - 1] / trades)


def solution(mesh):
    in_specs = (
        P("trade", "node"),
        P(None, "node"),
        P(None, "node"),
        P(None, "node"),
        P(None, "node"),
        P(None, "node"),
        P("node"),
        P("trade", None),
        P("trade"),
        P("trade"),
        P(),
    )
    out_specs = (P(("trade", "node"), None), P(("trade", "node")), P())
    body = functools.partial(local, mesh.shape["node"], mesh.shape["trade"])
    return jax.shard_map(body, mesh=mesh, in_specs=in_specs, out_specs=out_specs, check_vma=False)
```

time: 176 us -> 75.1 us (0.43)
  Pallas kernels: 0 us -> 60.3 us
  waiting for transfers between devices: 54.1 us -> 0 us
  blocking collectives: 39.5 us -> 0 us
  other arithmetic: 24.9 us -> 0 us
  local copies, waits for them, and re-layouts: 35.1 us -> 11.9 us
  between operations: 16.2 us -> 2.45 us
  starting transfers between devices: 5.38 us -> 0 us
    pallas_call x0 -> x1, Pallas kernels: none -> 60.3 us  [local(): pl.pallas_call(functools.partial(kernel, n, trade_count), out_shape=(jax....]
    psum x1 -> x0, blocking collectives: 39.5 us -> none  [local(): lax.psum(jnp.sum(prices), ('trade', 'node')) / values_in.shape[0]]
    all_to_all x1 -> x0, waiting for transfers between devices: 34.6 us -> none  [to_trade_rows(): lax.all_to_all(blocks, 'node', split_axis=0, concat_axis=2, tiled=True)]
    slice x5 -> x1, local copies, waits for them, and re-layouts: 25.2 us -> 0.58 us  [local(): return (values, small[0, :rows], small[0, LANES - 1] / trades)]
    select_n x15 -> x0, other arithmetic: 21.1 us -> none  [exercise(): return jnp.where(active[:, None], jnp.maximum(values, payoff), values)]
    all_gather x1 -> x0, waiting for transfers between devices: 19.5 us -> none  [local(): lattice = lax.all_gather(local_lattice, 'node', axis=2, tiled=True)]
    all_to_all x1 -> x0, starting transfers between devices: 5.34 us -> none  [to_trade_rows(): lax.all_to_all(blocks, 'node', split_axis=0, concat_axis=2, tiled=True)]
    reduce_sum x2 -> x0, other arithmetic: 3.47 us -> none  [the longest x1 3.38 us: local(): jnp.sum(prices)]
  transfers between devices with their start and end apart: 2 -> 0, of which waited for: 2 -> 0; matrix products, arithmetic and copies ran while one was open for 1% -> 0% of each run, Pallas kernels for 0% -> 0%
where the time goes in v1:
time: 75.1 us; the launch traced here: 74.7 us
  Pallas kernels  60.3 us (80%)
  local copies, waits for them, and re-layouts  11.9 us (16%)
  between operations  2.45 us (3%)
    pallas_call x1, Pallas kernels, local(): pl.pallas_call(functools.partial(kernel, n, trade_count), out_shape=(jax....  60.3 us
    unnamed x23, local copies, waits for them, and re-layouts  10.8 us

profile of v1, /device:TPU:0, one launch (start us, length us, event | category | flops | bytes accessed | tf_op | source)
XLA Modules:
  0.0 74.7 jit_solution(943053894997402504)
XLA Ops:
  0.6 0.0 copy-start
  0.6 1.6 %copy-done = f32[256,2048]{1,0:T(8,128)S(1)} copy-done((f32[256,2048]{1,0:T(8,128)S(1)}, f32[256,2048]{1,0:T(8,128)}, u32[]{:S(2)}) %copy-start) | copy-done | bytes 2097176
  2.2 0.0 copy-start.1
  2.2 0.9 %copy-done.1 = f32[16,2048]{1,0:T(8,128)S(1)} copy-done((f32[16,2048]{1,0:T(8,128)S(1)}, f32[16,2048]{1,0:T(8,128)}, u32[]{:S(2)}) %copy-start.1) | copy-done | bytes 131096
  3.1 0.0 copy-start.2
  3.1 0.9 %copy-done.2 = f32[16,2048]{1,0:T(8,128)S(1)} copy-done((f32[16,2048]{1,0:T(8,128)S(1)}, f32[16,2048]{1,0:T(8,128)}, u32[]{:S(2)}) %copy-start.2) | copy-done | bytes 131096
  4.0 0.0 copy-start.3
  4.0 0.9 %copy-done.3 = f32[16,2048]{1,0:T(8,128)S(1)} copy-done((f32[16,2048]{1,0:T(8,128)S(1)}, f32[16,2048]{1,0:T(8,128)}, u32[]{:S(2)}) %copy-start.3) | copy-done | bytes 131096
  4.9 0.0 copy-start.4
  4.9 0.9 %copy-done.4 = f32[16,2048]{1,0:T(8,128)S(1)} copy-done((f32[16,2048]{1,0:T(8,128)S(1)}, f32[16,2048]{1,0:T(8,128)}, u32[]{:S(2)}) %copy-start.4) | copy-done | bytes 131096
  5.8 0.0 copy-start.5
  5.8 0.9 %copy-done.5 = f32[16,2048]{1,0:T(8,128)S(1)} copy-done((f32[16,2048]{1,0:T(8,128)S(1)}, f32[16,2048]{1,0:T(8,128)}, u32[]{:S(2)}) %copy-start.5) | copy-done | bytes 131096
  6.8 0.0 copy-start.6
  6.8 0.7 copy-done.6
  7.4 0.0 copy-start.7
  7.5 0.7 copy-done.7
  8.1 0.0 copy-start.8
  8.1 0.7 copy-done.8
  8.8 0.0 copy-start.9
  8.8 0.7 copy-done.9
  9.5 0.0 copy-start.10
  9.5 0.7 copy-done.10
  10.2 60.3 %shard_map.130 = (f32[32,16384]{1,0:T(8,128)S(1)}, f32[1,128]{1,0:T(1,128)S(1)}) custom-call(f32[256,2048]{1,0:T(8,128)S(1)} %copy-done, f32[16,2048]{1,0:T(8,128)S(1)} %copy-done.1, f32[16,2048]{1,0:T(8,128)S(1)} %copy-done.2, f32[16,2048]{1,0:T(8,128)S(1)} %copy-done.3, f32[16,2048]{1,0:T(8,128)S(1)} %copy-done.4, f32[16,2048]{1,0:T(8,128)S(1)} %copy-done.5, ...), custom_call_target="tpu_custom_call" | custom-call | tf_op jit(solution)/shard_map/pallas_call | solution.py:352
  70.5 0.5 slice_bitcast_fusion
  71.0 0.6 slice.7
  72.2 1.3 %copy.15 = f32[32,16384]{1,0:T(8,128)} copy(f32[32,16384]{1,0:T(8,128)S(1)} %get-tuple-element.10) | data formatting | bytes 4194304
Async XLA Ops:
  0.6 1.6 %copy-start = (f32[256,2048]{1,0:T(8,128)S(1)}, f32[256,2048]{1,0:T(8,128)}, u32[]{:S(2)}) copy-start(f32[256,2048]{1,0:T(8,128)} %values_hbm.1) | copy-start | bytes 6291460
  2.2 0.9 %copy-start.1 = (f32[16,2048]{1,0:T(8,128)S(1)}, f32[16,2048]{1,0:T(8,128)}, u32[]{:S(2)}) copy-start(f32[16,2048]{1,0:T(8,128)} %up_hbm.1) | copy-start | bytes 393220
  3.1 0.9 %copy-start.2 = (f32[16,2048]{1,0:T(8,128)S(1)}, f32[16,2048]{1,0:T(8,128)}, u32[]{:S(2)}) copy-start(f32[16,2048]{1,0:T(8,128)} %down_hbm.1) | copy-start | bytes 393220
  4.0 0.9 %copy-start.3 = (f32[16,2048]{1,0:T(8,128)S(1)}, f32[16,2048]{1,0:T(8,128)}, u32[]{:S(2)}) copy-start(f32[16,2048]{1,0:T(8,128)} %disc_hbm.1) | copy-start | bytes 393220
  4.9 0.9 %copy-start.4 = (f32[16,2048]{1,0:T(8,128)S(1)}, f32[16,2048]{1,0:T(8,128)}, u32[]{:S(2)}) copy-start(f32[16,2048]{1,0:T(8,128)} %swap_hbm.1) | copy-start | bytes 393220
  5.8 0.9 %copy-start.5 = (f32[16,2048]{1,0:T(8,128)S(1)}, f32[16,2048]{1,0:T(8,128)}, u32[]{:S(2)}) copy-start(f32[16,2048]{1,0:T(8,128)} %ann_hbm.1) | copy-start | bytes 393220
  6.8 0.7 copy-start.6
  7.4 0.7 copy-start.7
  8.1 0.7 copy-start.8
  8.8 0.7 copy-start.9
  9.5 0.7 copy-start.10

commit v2 on v1

--- a/solution.py
+++ b/solution.py
@@ -21,15 +21,20 @@
     disc_hbm,
     swap_hbm,
     ann_hbm,
+    price_hbm,
+    dates_hbm,
+    bucket_hbm,
+    sign_hbm,
+    table_hbm,
+    out_ref,
+    small_ref,
+    work,
+    lattice,
     price_ref,
     dates_ref,
     bucket_ref,
     sign_ref,
     table_ref,
-    out_ref,
-    small_ref,
-    work,
-    lattice,
     halo_values,
     halo_lattice,
     coef,
@@ -43,6 +48,7 @@
     msg_recv,
     in_sem,
     lat_sem,
+    trade_sem,
     self_sem,
     hv_send,
     hv_recv,
@@ -83,7 +89,19 @@
     lat_copies = [
         pltpu.make_async_copy(lat_hbm[i], lattice.at[i], lat_sem.at[i]) for i in range(5)
     ]
-    for copy in lat_copies:
+    trade_copies = [
+        pltpu.make_async_copy(source, held, trade_sem.at[i])
+        for i, (source, held) in enumerate(
+            (
+                (dates_hbm, dates_ref),
+                (bucket_hbm, bucket_ref),
+                (sign_hbm, sign_ref),
+                (table_hbm, table_ref),
+                (price_hbm, price_ref),
+            )
+        )
+    ]
+    for copy in trade_copies + lat_copies:
         copy.start()
     for turn in range(n):
         in_copy(turn).start()
@@ -130,6 +148,8 @@
     for copy in halos:
         copy.start()
 
+    for copy in trade_copies:
+        copy.wait()
     rows_t[0:4, :] = dates_ref[...].astype(jnp.float32)
     rows_t[4:5, :] = bucket_ref[...].astype(jnp.float32)
     rows_t[5:6, :] = sign_ref[...].astype(jnp.float32)
@@ -220,16 +240,17 @@
                 scale.append(jnp.where(active, signs[u], 0.0))
                 shift.append(jnp.where(active, strikes[u], 0.0))
             old = [flat[u * count : (u + 1) * count] for u in range(tiles)]
-            down = [[pltpu.roll(x, 1, 1) for x in old[u]] for u in range(tiles)]
-            up = [[pltpu.roll(x, LANES - 1, 1) for x in old[u]] for u in range(tiles)]
             new = [[] for _ in range(tiles)]
             for k in range(count):
                 a, b, c = coef[0, step, k], coef[1, step, k], coef[2, step, k]
                 pay, ann = coef[3, step, k], coef[4, step, k]
                 for u in range(tiles):
-                    above = jnp.where(is_last, up[u][(k + 1) % count], up[u][k])
-                    below = jnp.where(is_first, down[u][k - 1], down[u][k])
-                    rolled = a * above + b * old[u][k] + c * below
+                    x = old[u]
+                    above = pltpu.roll(
+                        jnp.where(is_first, x[(k + 1) % count], x[k]), LANES - 1, 1
+                    )
+                    below = pltpu.roll(jnp.where(is_last, x[k - 1], x[k]), 1, 1)
+                    rolled = a * above + b * x[k] + c * below
                     new[u].append(jnp.maximum(rolled, scale[u] * pay - shift[u] * ann))
             return tuple(x for u in range(tiles) for x in new[u])
 
@@ -321,7 +342,8 @@
     for turn in range(n - 1):
         msg_copy(turn).wait()
         result = result + msg_recv[turn]
-    small_ref[...] = jnp.sum(result, axis=0, keepdims=True)
+    prices = jnp.sum(result, axis=0, keepdims=True)
+    small_ref[...] = prices * jnp.where(lane[:1] == LANES - 1, 1.0 / trades, 1.0)
     for turn in range(n - 1):
         block_copy(turn).wait()
 
@@ -347,7 +369,7 @@
     rows = trades // n
     f32 = jnp.float32
     dma = pltpu.SemaphoreType.DMA
-    any_spec = pl.BlockSpec(memory_space=pl.ANY)
+    hbm_spec = pl.BlockSpec(memory_space=pltpu.HBM)
     vmem_spec = pl.BlockSpec(memory_space=pltpu.VMEM)
     values, small = pl.pallas_call(
         functools.partial(kernel, n, trade_count),
@@ -355,11 +377,16 @@
             jax.ShapeDtypeStruct((rows, width * n), f32),
             jax.ShapeDtypeStruct((1, LANES), f32),
         ),
-        in_specs=[any_spec] * 6 + [vmem_spec] * 5,
-        out_specs=(vmem_spec, vmem_spec),
+        in_specs=[hbm_spec] * 11,
+        out_specs=(hbm_spec, vmem_spec),
         scratch_shapes=[
             pltpu.VMEM((trades, width), f32),
             pltpu.VMEM((5, steps, width), f32),
+            pltpu.VMEM((1, width), f32),
+            pltpu.VMEM((4, trades), jnp.int32),
+            pltpu.VMEM((1, trades), jnp.int32),
+            pltpu.VMEM((1, trades), jnp.int32),
+            pltpu.VMEM((1, strike_table.shape[0]), f32),
             pltpu.VMEM((2, trades, LANES), f32),
             pltpu.VMEM((2, 5, steps, LANES), f32),
             pltpu.VMEM((5, steps, width // LANES + 1, SUB, LANES), f32),
@@ -372,6 +399,7 @@
             pltpu.VMEM((n, SUB, LANES), f32),
             pltpu.VMEM((n - 1, SUB, LANES), f32),
             dma((n,)),
+            dma((5,)),
             dma((5,)),
             dma,
             dma((2,)),
@@ -386,7 +414,7 @@
             dma((n - 1,)),
         ],
         compiler_params=pltpu.CompilerParams(
-            collective_id=0, has_side_effects=True, vmem_limit_bytes=32 * 1024 * 1024
+            collective_id=0, has_side_effects=True, vmem_limit_bytes=67043328
         ),
     )(
         values_in,
@@ -401,7 +429,7 @@
         notional_sign.reshape(1, trades),
         strike_table.reshape(1, strike_table.shape[0]),
     )
-    return (values, small[0, :rows], small[0, LANES - 1] / trades)
+    return (values, small[0, :rows], small[0, LANES - 1])
 
 
 def solution(mesh):

time: 75.1 us -> 62.7 us (0.83)
  local copies, waits for them, and re-layouts: 11.9 us -> 5.4 us
  Pallas kernels: 60.3 us -> 56.5 us
  between operations: 2.45 us -> 0.64 us
    unnamed x23 -> x1, local copies, waits for them, and re-layouts: 10.8 us -> 3.04 us
    pallas_call x1, Pallas kernels: 60.3 us -> 56.5 us  [local(): pl.pallas_call(functools.partial(kernel, n, trade_count), out_shape=(jax....]
where the time goes in v2:
time: 62.7 us; the launch traced here: 62.6 us
  Pallas kernels  56.5 us (90%)
  local copies, waits for them, and re-layouts  5.4 us (9%)
  between operations  0.64 us (1%)
    pallas_call x1, Pallas kernels, local(): pl.pallas_call(functools.partial(kernel, n, trade_count), out_shape=(jax....  56.5 us
    unnamed x1, local copies, waits for them, and re-layouts  3.04 us

profile of v2, /device:TPU:0, one launch (start us, length us, event | category | flops | bytes accessed | tf_op | source)
XLA Modules:
  0.0 62.6 jit_solution(18435588697706752985)
XLA Ops:
  0.6 56.5 %shard_map.130 = (f32[32,16384]{1,0:T(8,128)}, f32[1,128]{1,0:T(1,128)}) custom-call(f32[256,2048]{1,0:T(8,128)} %values_hbm.1, f32[16,2048]{1,0:T(8,128)} %up_hbm.1, f32[16,2048]{1,0:T(8,128)} %down_hbm.1, f32[16,2048]{1,0:T(8,128)} %disc_hbm.1, f32[16,2048]{1,0:T(8,128)} %swap_hbm.1, f32[16,2048]{1,0:T(8,128)} %ann_hbm.1, f32[1,2048]{1,0:T(1,128)} %bitcast.8, ...), custom_call_target="tpu_custom_call" | custom-call | tf_op jit(solution)/shard_map/pallas_call | solution.py:374
  57.1 1.1 %slice_bitcast_fusion = f32[32]{0:T(128)} fusion(f32[1,128]{1,0:T(1,128)} %get-tuple-element.6), kind=kLoop, calls=%fused_computation | loop fusion | bytes 256 | tf_op jit(solution)/shard_map/squeeze | solution.py:432
  58.3 1.2 %slice.7 = f32[1,1]{1,0:T(1,128)} slice(f32[1,128]{1,0:T(1,128)} %get-tuple-element.6), slice={[0:1], [127:128]} | slice | bytes 8 | tf_op jit(solution)/shard_map/slice | solution.py:432
  59.5 3.0 %copy.15 = f32[32,16384]{1,0:T(8,128)} copy(f32[32,16384]{1,0:T(8,128)} %get-tuple-element.10) | data formatting | bytes 4194304
